TPU v7x, 32 devices: a whole 2x2x4 slice. The times are simulated.
32 devices in a mesh: rows: 16 (over z, y, core), cols: 2 (over x).
Axes of the slice: x: 2, y: 2, z: 4, core: 2. Of those that a mesh axis runs over, the one named last changes fastest.
Arguments:
- design: bfloat16 [32768, 6144], P('rows', 'cols'), may hold values from -0.03125 to 0.03125
- targets: bfloat16 [32768, 128], P('rows'), may hold values from -6 to 6
- col_scale: float32 [6144], P('cols'), may hold values from 0.1 to 1
Outputs:
- solution: float32 [6144, 128], P('cols', 'rows')
- residual: float32 [32768, 128], P('rows')
All inputs are finite; a program needn't handle non-finite values.
Results may differ from a plain program's by a relative error of at most 0.0065.
Values may be sent and summed in bfloat16 or wider, within the bound.
A program may use at most 128 MiB of HBM per device.

v0:
```python
import jax
import jax.numpy as jnp
from jax import lax
from jax.sharding import PartitionSpec as P

ITERS = 6


def local_back(design, vectors):
    return lax.dot_general(
        design, vectors, (((0,), (0,)), ((), ())), preferred_element_type=jnp.float32
    )


def per_device(design, targets, col_scale):
    fits = targets.shape[1]
    row_count = lax.axis_size("rows")
    residual = targets.astype(jnp.float32)
    scale = col_scale[:, None]

    def gradient_of(vectors):
        return scale * lax.psum(local_back(design, vectors), "rows")

    def squared(values):
        return lax.psum(jnp.sum(values * values, axis=0), "cols")

    gradient = gradient_of(targets)
    gamma = squared(gradient)
    solution = jnp.zeros(gradient.shape, jnp.float32)
    direction = gradient
    for step in range(ITERS):
        scaled_dir = (scale * direction).astype(jnp.bfloat16)
        image = lax.psum(
            jnp.dot(design, scaled_dir, preferred_element_type=jnp.float32).astype(jnp.bfloat16),
            "cols",
        ).astype(jnp.float32)
        delta = lax.psum(jnp.sum(image * image, axis=0), "rows")
        alpha = gamma / delta
        solution = solution + alpha * direction
        residual = residual - alpha * image
        if step + 1 < ITERS:
            gradient = gradient_of(residual.astype(jnp.bfloat16))
            gamma_new = squared(gradient)
            direction = gradient + gamma_new / gamma * direction
            gamma = gamma_new
    own = fits // row_count
    solution_part = lax.dynamic_slice_in_dim(solution, lax.axis_index("rows") * own, own, 1)
    return (solution_part, residual)


def solution(mesh):
    in_specs = (P("rows", "cols"), P("rows", None), P("cols"))
    out_specs = (P("cols", "rows"), P("rows", None))
    return jax.shard_map(
        per_device, mesh=mesh, in_specs=in_specs, out_specs=out_specs, check_vma=False
    )
```

profile of v0, /device:TPU:0, one launch (start us, length us, event | category | flops | bytes accessed | tf_op | source)
XLA Modules:
  0.0 1142.6 jit_solution(10677562298321157389)
XLA Ops:
  7.2 9.3 fusion.42
  16.5 98.8 %all-reduce.13.cloned.1.call-done = f32[3072,128]{1,0:T(8,128)} async-done(((f32[3072,128]{1,0:T(8,128)}), f32[3072,128]{1,0:T(8,128)}) %all-reduce.13.cloned.1.call-update) | async-done | bytes 1572880 | tf_op jit(solution)/shard_map/psum | solution.py:22
  117.2 10.4 fusion
  127.9 4.9 psum.169
  132.8 22.5 %all-reduce.15.cloned.1.call-done = bf16[2048,128]{0,1:T(8,128)(2,1)} async-done(((bf16[2048,128]{0,1:T(8,128)(2,1)}), bf16[2048,128]{0,1:T(8,128)(2,1)}) %all-reduce.15.cloned.1.call-update) | async-done | bytes 524304 | tf_op jit(solution)/shard_map/psum | solution.py:33
  156.5 33.2 %psum.171 = f32[128]{0:T(128)S(1)} all-reduce(f32[128]{0:T(128)S(1)} %fusion.11), channel_id=1, replica_groups=mesh['rows'=16,'cols'=2] {'rows'}, use_global_device_ids=true, to_apply=%region_5.0 | all-reduce | flops 128 | bytes 1024 | tf_op jit(solution)/shard_map/psum | solution.py:37
  189.8 11.0 convolution_bitcast_fusion.4
  200.8 92.3 %all-reduce.17.cloned.1.call-done = f32[3072,128]{1,0:T(8,128)} async-done(((f32[3072,128]{1,0:T(8,128)}), f32[3072,128]{1,0:T(8,128)}) %all-reduce.17.cloned.1.call-update) | async-done | bytes 1572880 | tf_op jit(solution)/shard_map/psum | solution.py:22
  301.9 10.3 fusion.1
  312.2 27.6 %all-reduce.19.cloned.1.call-done = bf16[2048,128]{0,1:T(8,128)(2,1)} async-done(((bf16[2048,128]{0,1:T(8,128)(2,1)}), bf16[2048,128]{0,1:T(8,128)(2,1)}) %all-reduce.19.cloned.1.call-update) | async-done | bytes 524304 | tf_op jit(solution)/shard_map/psum | solution.py:33
  341.1 33.4 %psum.175 = f32[128]{0:T(128)S(1)} all-reduce(f32[128]{0:T(128)S(1)} %fusion.13), channel_id=1, replica_groups=mesh['rows'=16,'cols'=2] {'rows'}, use_global_device_ids=true, to_apply=%region_11.0 | all-reduce | flops 128 | bytes 1024 | tf_op jit(solution)/shard_map/psum | solution.py:37
  374.5 11.3 convolution_bitcast_fusion.3
  385.9 92.3 %all-reduce.21.cloned.1.call-done = f32[3072,128]{1,0:T(8,128)} async-done(((f32[3072,128]{1,0:T(8,128)}), f32[3072,128]{1,0:T(8,128)}) %all-reduce.21.cloned.1.call-update) | async-done | bytes 1572880 | tf_op jit(solution)/shard_map/psum | solution.py:22
  488.1 10.3 fusion.2
  498.5 27.6 %all-reduce.23.cloned.1.call-done = bf16[2048,128]{0,1:T(8,128)(2,1)} async-done(((bf16[2048,128]{0,1:T(8,128)(2,1)}), bf16[2048,128]{0,1:T(8,128)(2,1)}) %all-reduce.23.cloned.1.call-update) | async-done | bytes 524304 | tf_op jit(solution)/shard_map/psum | solution.py:33
  527.4 33.2 %psum.179 = f32[128]{0:T(128)S(1)} all-reduce(f32[128]{0:T(128)S(1)} %fusion.15), channel_id=1, replica_groups=mesh['rows'=16,'cols'=2] {'rows'}, use_global_device_ids=true, to_apply=%region_17.0 | all-reduce | flops 128 | bytes 1024 | tf_op jit(solution)/shard_map/psum | solution.py:37
  560.6 11.5 %convolution_bitcast_fusion.2 = f32[3072,128]{1,0:T(8,128)} fusion(bf16[2048,3072]{1,0:T(8,128)(2,1)} %param.3, bf16[2048,128]{0,1:T(8,128)(2,1)} %all-reduce.23.cloned.1.call-done, f32[128]{0:T(128)S(1)} %div.37, bf16[2048,128]{0,1:T(8,128)(2,1)} %all-reduce.19.cloned.1.call-done, bf16[2048,128]{0,1:T(8,128)(2,1)} %all-reduce.15.cloned.1.call-done, ...), kind=kOutput, calls=%fused_computation.2 | convolution fusion | flops 1613496320 | bytes 16254464 | tf_op jit(solution)/shard_map/dot_general | solution.py:10
  572.2 92.0 %all-reduce.25.cloned.1.call-done = f32[3072,128]{1,0:T(8,128)} async-done(((f32[3072,128]{1,0:T(8,128)}), f32[3072,128]{1,0:T(8,128)}) %all-reduce.25.cloned.1.call-update) | async-done | bytes 1572880 | tf_op jit(solution)/shard_map/psum | solution.py:22
  674.5 10.3 fusion.3
  684.9 27.6 %all-reduce.27.cloned.1.call-done = bf16[2048,128]{0,1:T(8,128)(2,1)} async-done(((bf16[2048,128]{0,1:T(8,128)(2,1)}), bf16[2048,128]{0,1:T(8,128)(2,1)}) %all-reduce.27.cloned.1.call-update) | async-done | bytes 524304 | tf_op jit(solution)/shard_map/psum | solution.py:33
  713.8 33.2 %psum.183 = f32[128]{0:T(128)S(1)} all-reduce(f32[128]{0:T(128)S(1)} %fusion.17), channel_id=1, replica_groups=mesh['rows'=16,'cols'=2] {'rows'}, use_global_device_ids=true, to_apply=%region_23.0 | all-reduce | flops 128 | bytes 1024 | tf_op jit(solution)/shard_map/psum | solution.py:37
  750.3 9.1 convolution_bitcast_fusion.1
  759.4 92.2 %all-reduce.29.cloned.1.call-done = f32[3072,128]{1,0:T(8,128)} async-done(((f32[3072,128]{1,0:T(8,128)}), f32[3072,128]{1,0:T(8,128)}) %all-reduce.29.cloned.1.call-update) | async-done | bytes 1572880 | tf_op jit(solution)/shard_map/psum | solution.py:22
  861.9 10.3 fusion.4
  872.3 27.6 %all-reduce.31.cloned.1.call-done = bf16[2048,128]{0,1:T(8,128)(2,1)} async-done(((bf16[2048,128]{0,1:T(8,128)(2,1)}), bf16[2048,128]{0,1:T(8,128)(2,1)}) %all-reduce.31.cloned.1.call-update) | async-done | bytes 524304 | tf_op jit(solution)/shard_map/psum | solution.py:33
  901.2 33.3 %psum.187 = f32[128]{0:T(128)S(1)} all-reduce(f32[128]{0:T(128)S(1)} %fusion.19), channel_id=1, replica_groups=mesh['rows'=16,'cols'=2] {'rows'}, use_global_device_ids=true, to_apply=%region_29.0 | all-reduce | flops 128 | bytes 1024 | tf_op jit(solution)/shard_map/psum | solution.py:37
  934.5 11.3 convolution_bitcast_fusion
  945.8 92.0 %all-reduce.33.cloned.1.call-done = f32[3072,128]{1,0:T(8,128)} async-done(((f32[3072,128]{1,0:T(8,128)}), f32[3072,128]{1,0:T(8,128)}) %all-reduce.33.cloned.1.call-update) | async-done | bytes 1572880 | tf_op jit(solution)/shard_map/psum | solution.py:22
  1048.2 10.3 fusion.5
  1058.9 27.3 %all-reduce.35.cloned.1.call-done = bf16[2048,128]{0,1:T(8,128)(2,1)} async-done(((bf16[2048,128]{0,1:T(8,128)(2,1)}), bf16[2048,128]{0,1:T(8,128)(2,1)}) %all-reduce.35.cloned.1.call-update) | async-done | bytes 524304 | tf_op jit(solution)/shard_map/psum | solution.py:33
  1087.5 33.3 %psum.191 = f32[128]{0:T(128)S(1)} all-reduce(f32[128]{0:T(128)S(1)} %fusion.21), channel_id=1, replica_groups=mesh['rows'=16,'cols'=2] {'rows'}, use_global_device_ids=true, to_apply=%region_35.0 | all-reduce | flops 128 | bytes 1024 | tf_op jit(solution)/shard_map/psum | solution.py:37
  1126.3 6.5 fusion.6
  (84 shorter events, 71.3 us)
Async XLA Ops:
  7.2 108.2 %all-reduce.13.cloned.1.call-start = ((), (), s32[]{:S(2)}) async-start(), calls=%async_computation | async-start | bytes 3145728 | tf_op jit(solution)/shard_map/psum | solution.py:22
  16.5 98.9 %copy-start.6 = (f32[3072]{0:T(1024)S(1)}, f32[3072]{0:T(1024)}, u32[]{:S(2)}) copy-start(f32[3072]{0:T(1024)} %param.5) | copy-start | bytes 36868
  16.5 138.8 %all-reduce.15.cloned.1.call-start = ((), (), s32[]{:S(2)}) async-start(), calls=%async_computation.1 | async-start | bytes 1048576 | tf_op jit(solution)/shard_map/psum | solution.py:33
  117.2 10.4 copy-start.7
  127.6 165.5 %all-reduce.17.cloned.1.call-start = ((), (), s32[]{:S(2)}) async-start(), calls=%async_computation.2 | async-start | bytes 3145728 | tf_op jit(solution)/shard_map/psum | solution.py:22
  127.9 72.8 %copy-start.5 = (bf16[2048,128]{0,1:T(8,128)(2,1)}, bf16[2048,128]{0,1:T(8,128)(2,1)S(1)}, u32[]{:S(2)}) copy-start(bf16[2048,128]{0,1:T(8,128)(2,1)S(1)} %copy.5) | copy-start | bytes 1572868
  200.7 139.1 %all-reduce.19.cloned.1.call-start = ((), (), s32[]{:S(2)}) async-start(), calls=%async_computation.3 | async-start | bytes 1048576 | tf_op jit(solution)/shard_map/psum | solution.py:33
  312.2 166.1 %all-reduce.21.cloned.1.call-start = ((), (), s32[]{:S(2)}) async-start(), calls=%async_computation.4 | async-start | bytes 3145728 | tf_op jit(solution)/shard_map/psum | solution.py:22
  385.9 140.3 %all-reduce.23.cloned.1.call-start = ((), (), s32[]{:S(2)}) async-start(), calls=%async_computation.5 | async-start | bytes 1048576 | tf_op jit(solution)/shard_map/psum | solution.py:33
  487.0 1.2 copy-start
  498.5 165.7 %all-reduce.25.cloned.1.call-start = ((), (), s32[]{:S(2)}) async-start(), calls=%async_computation.6 | async-start | bytes 3145728 | tf_op jit(solution)/shard_map/psum | solution.py:22
  572.1 140.4 %all-reduce.27.cloned.1.call-start = ((), (), s32[]{:S(2)}) async-start(), calls=%async_computation.7 | async-start | bytes 1048576 | tf_op jit(solution)/shard_map/psum | solution.py:33
  673.4 1.1 copy-start.1
  684.9 166.7 %all-reduce.29.cloned.1.call-start = ((), (), s32[]{:S(2)}) async-start(), calls=%async_computation.8 | async-start | bytes 3145728 | tf_op jit(solution)/shard_map/psum | solution.py:22
  749.3 1.0 copy-start.3
  759.4 140.6 %all-reduce.31.cloned.1.call-start = ((), (), s32[]{:S(2)}) async-start(), calls=%async_computation.9 | async-start | bytes 1048576 | tf_op jit(solution)/shard_map/psum | solution.py:33
  860.8 1.1 copy-start.2
  872.3 165.6 %all-reduce.33.cloned.1.call-start = ((), (), s32[]{:S(2)}) async-start(), calls=%async_computation.10 | async-start | bytes 3145728 | tf_op jit(solution)/shard_map/psum | solution.py:22
  945.7 140.5 %all-reduce.35.cloned.1.call-start = ((), (), s32[]{:S(2)}) async-start(), calls=%async_computation.11 | async-start | bytes 1048576 | tf_op jit(solution)/shard_map/psum | solution.py:33
  1047.0 1.2 copy-start.4
Sparse Core Ops, SparseCore 0:
  16.6 98.6 all-reduce.12
  127.7 27.5 all-reduce.14
  200.9 92.2 all-reduce.16
  312.3 27.5 all-reduce.18
  386.0 92.2 all-reduce.20
  498.6 27.5 all-reduce.22
  572.2 91.9 all-reduce.24
  685.0 27.5 all-reduce.26
  759.5 92.0 all-reduce.28
  872.4 27.5 all-reduce.30
  945.9 91.9 all-reduce.32
  1058.7 27.5 all-reduce.34
where the time goes:
time: 1150 us; the launch traced here: 1140 us
  waiting for transfers between devices  720 us (63%)
  blocking collectives  229 us (20%)
  matrix products  125 us (11%)
  other arithmetic  41.2 us (4%)
  between operations  14.8 us (1%)
    psum x6, waiting for transfers between devices, gradient_of(): return scale * lax.psum(local_back(design, vectors), 'rows')  560 us
    psum x6, blocking collectives, per_device(): delta = lax.psum(jnp.sum(image * image, axis=0), 'rows')  200 us
    psum x6, waiting for transfers between devices, per_device(): lax.psum(jnp.dot(design, scaled_dir, preferred_element_type=jnp.float32)....  160 us
    dot_general x6, matrix products, local_back(): lax.dot_general(design, vectors, (((0,), (0,)), ((), ())), preferred_elem...  63.3 us
    dot_general x6, matrix products, per_device(): jnp.dot(design, scaled_dir, preferred_element_type=jnp.float32)  61.9 us
    psum x6, blocking collectives, squared(): return lax.psum(jnp.sum(values * values, axis=0), 'cols')  29.6 us
  transfers between devices with their start and end apart: 12, of which 12 were waited for; matrix products, arithmetic and copies ran while one was open for 0% of the time, Pallas kernels for 0%

commit v1 on v0

--- a/solution.py
+++ b/solution.py
@@ -34,7 +34,9 @@
             jnp.dot(design, scaled_dir, preferred_element_type=jnp.float32).astype(jnp.bfloat16),
             "cols",
         ).astype(jnp.float32)
-        delta = lax.psum(jnp.sum(image * image, axis=0), "rows")
+        packet = jnp.sum(image * image, axis=0)
+        back = jax.lax.all_gather(packet, "rows")
+        delta = jnp.sum(back, axis=0)
         alpha = gamma / delta
         solution = solution + alpha * direction
         residual = residual - alpha * image

time: 1150 us -> 1080 us (0.939)
  blocking collectives: 229 us -> 159 us
    psum x6 -> x0, blocking collectives: 200 us -> none  [per_device(): delta = lax.psum(jnp.sum(image * image, axis=0), 'rows')]
    all_gather x0 -> x6, blocking collectives: none -> 130 us  [per_device(): back = jax.lax.all_gather(packet, 'rows')]
where the time goes in v1:
time: 1080 us; the launch traced here: 1070 us
  waiting for transfers between devices  721 us (67%)
  blocking collectives  159 us (15%)
  matrix products  125 us (12%)
  other arithmetic  41.4 us (4%)
  between operations  14.8 us (1%)
  local copies, waits for them, and re-layouts  11.2 us (1%)
    psum x6, waiting for transfers between devices, gradient_of(): return scale * lax.psum(local_back(design, vectors), 'rows')  560 us
    psum x6, waiting for transfers between devices, per_device(): lax.psum(jnp.dot(design, scaled_dir, preferred_element_type=jnp.float32)....  160 us
    all_gather x6, blocking collectives, per_device(): back = jax.lax.all_gather(packet, 'rows')  130 us
    dot_general x6, matrix products, local_back(): lax.dot_general(design, vectors, (((0,), (0,)), ((), ())), preferred_elem...  63.3 us
    dot_general x6, matrix products, per_device(): jnp.dot(design, scaled_dir, preferred_element_type=jnp.float32)  61.9 us
    psum x6, blocking collectives, squared(): return lax.psum(jnp.sum(values * values, axis=0), 'cols')  29.6 us
  transfers between devices with their start and end apart: 12, of which 12 were waited for; matrix products, arithmetic and copies ran while one was open for 0% of the time, Pallas kernels for 0%

profile of v1, /device:TPU:0, one launch (start us, length us, event | category | flops | bytes accessed | tf_op | source)
XLA Modules:
  0.0 1072.9 jit_solution(10363548127557364346)
XLA Ops:
  7.2 9.3 fusion.42
  16.5 98.8 %all-reduce.13.cloned.1.call-done = f32[3072,128]{1,0:T(8,128)} async-done(((f32[3072,128]{1,0:T(8,128)}), f32[3072,128]{1,0:T(8,128)}) %all-reduce.13.cloned.1.call-update) | async-done | bytes 1572880 | tf_op jit(solution)/shard_map/psum | solution.py:22
  117.2 10.4 fusion
  127.9 4.9 psum.127
  132.8 22.5 %all-reduce.15.cloned.1.call-done = bf16[2048,128]{0,1:T(8,128)(2,1)} async-done(((bf16[2048,128]{0,1:T(8,128)(2,1)}), bf16[2048,128]{0,1:T(8,128)(2,1)}) %all-reduce.15.cloned.1.call-update) | async-done | bytes 524304 | tf_op jit(solution)/shard_map/psum | solution.py:33
  156.5 21.5 %all-gather.6 = f32[16,1,128]{2,1,0:T(1,128)S(1)} all-gather(f32[1,1,128]{2,1,0:T(1,128)S(1)} %bitcast.41), channel_id=2, replica_groups=mesh['rows'=16,'cols'=2] {'rows'}, dimensions={0}, use_global_device_ids=true | all-gather | bytes 8704 | tf_op jit(solution)/shard_map/all_gather | solution.py:38
  178.1 11.0 %convolution_bitcast_fusion.4 = f32[3072,128]{1,0:T(8,128)} fusion(bf16[2048,3072]{1,0:T(8,128)(2,1)} %param.3, bf16[2048,128]{0,1:T(8,128)(2,1)} %all-reduce.15.cloned.1.call-done, bf16[2048,128]{0,1:T(8,128)(2,1)S(1)} %copy.13, f32[128]{0:T(128)S(1)} %div.33), kind=kOutput, calls=%fused_computation.4 | convolution fusion | flops 1611923456 | bytes 15204864 | tf_op jit(solution)/shard_map/dot_general | solution.py:10
  189.1 92.4 %all-reduce.17.cloned.1.call-done = f32[3072,128]{1,0:T(8,128)} async-done(((f32[3072,128]{1,0:T(8,128)}), f32[3072,128]{1,0:T(8,128)}) %all-reduce.17.cloned.1.call-update) | async-done | bytes 1572880 | tf_op jit(solution)/shard_map/psum | solution.py:22
  290.2 10.3 fusion.1
  300.6 27.6 %all-reduce.19.cloned.1.call-done = bf16[2048,128]{0,1:T(8,128)(2,1)} async-done(((bf16[2048,128]{0,1:T(8,128)(2,1)}), bf16[2048,128]{0,1:T(8,128)(2,1)}) %all-reduce.19.cloned.1.call-update) | async-done | bytes 524304 | tf_op jit(solution)/shard_map/psum | solution.py:33
  329.5 21.7 %all-gather.7 = f32[16,1,128]{2,1,0:T(1,128)S(1)} all-gather(f32[1,1,128]{2,1,0:T(1,128)S(1)} %bitcast.42), channel_id=3, replica_groups=mesh['rows'=16,'cols'=2] {'rows'}, dimensions={0}, use_global_device_ids=true | all-gather | bytes 8704 | tf_op jit(solution)/shard_map/all_gather | solution.py:38
  351.3 11.3 %convolution_bitcast_fusion.3 = f32[3072,128]{1,0:T(8,128)} fusion(bf16[2048,3072]{1,0:T(8,128)(2,1)} %param.3, bf16[2048,128]{0,1:T(8,128)(2,1)} %all-reduce.19.cloned.1.call-done, bf16[2048,128]{0,1:T(8,128)(2,1)} %all-reduce.15.cloned.1.call-done, bf16[2048,128]{0,1:T(8,128)(2,1)} %copy-done.5, f32[128]{0:T(128)S(1)} %div.35, f32[128]{0:T(128)S(1)} %div.33), kind=kOutput, calls=%fused_computation.3 | convolution fusion | flops 1612709888 | bytes 15729664 | tf_op jit(solution)/shard_map/dot_general | solution.py:10
  362.6 92.4 %all-reduce.21.cloned.1.call-done = f32[3072,128]{1,0:T(8,128)} async-done(((f32[3072,128]{1,0:T(8,128)}), f32[3072,128]{1,0:T(8,128)}) %all-reduce.21.cloned.1.call-update) | async-done | bytes 1572880 | tf_op jit(solution)/shard_map/psum | solution.py:22
  464.9 10.3 fusion.2
  475.2 27.6 %all-reduce.23.cloned.1.call-done = bf16[2048,128]{0,1:T(8,128)(2,1)} async-done(((bf16[2048,128]{0,1:T(8,128)(2,1)}), bf16[2048,128]{0,1:T(8,128)(2,1)}) %all-reduce.23.cloned.1.call-update) | async-done | bytes 524304 | tf_op jit(solution)/shard_map/psum | solution.py:33
  504.1 21.5 %all-gather.8 = f32[16,1,128]{2,1,0:T(1,128)S(1)} all-gather(f32[1,1,128]{2,1,0:T(1,128)S(1)} %bitcast.43), channel_id=4, replica_groups=mesh['rows'=16,'cols'=2] {'rows'}, dimensions={0}, use_global_device_ids=true | all-gather | bytes 8704 | tf_op jit(solution)/shard_map/all_gather | solution.py:38
  525.7 11.5 %convolution_bitcast_fusion.2 = f32[3072,128]{1,0:T(8,128)} fusion(bf16[2048,3072]{1,0:T(8,128)(2,1)} %param.3, bf16[2048,128]{0,1:T(8,128)(2,1)} %all-reduce.23.cloned.1.call-done, f32[128]{0:T(128)S(1)} %div.37, bf16[2048,128]{0,1:T(8,128)(2,1)} %all-reduce.19.cloned.1.call-done, bf16[2048,128]{0,1:T(8,128)(2,1)} %all-reduce.15.cloned.1.call-done, ...), kind=kOutput, calls=%fused_computation.2 | convolution fusion | flops 1613496320 | bytes 16254464 | tf_op jit(solution)/shard_map/dot_general | solution.py:10
  537.2 92.1 %all-reduce.25.cloned.1.call-done = f32[3072,128]{1,0:T(8,128)} async-done(((f32[3072,128]{1,0:T(8,128)}), f32[3072,128]{1,0:T(8,128)}) %all-reduce.25.cloned.1.call-update) | async-done | bytes 1572880 | tf_op jit(solution)/shard_map/psum | solution.py:22
  639.6 10.3 fusion.3
  650.0 27.6 %all-reduce.27.cloned.1.call-done = bf16[2048,128]{0,1:T(8,128)(2,1)} async-done(((bf16[2048,128]{0,1:T(8,128)(2,1)}), bf16[2048,128]{0,1:T(8,128)(2,1)}) %all-reduce.27.cloned.1.call-update) | async-done | bytes 524304 | tf_op jit(solution)/shard_map/psum | solution.py:33
  678.9 21.5 %all-gather.9 = f32[16,1,128]{2,1,0:T(1,128)S(1)} all-gather(f32[1,1,128]{2,1,0:T(1,128)S(1)} %bitcast.44), channel_id=5, replica_groups=mesh['rows'=16,'cols'=2] {'rows'}, dimensions={0}, use_global_device_ids=true | all-gather | bytes 8704 | tf_op jit(solution)/shard_map/all_gather | solution.py:38
  703.7 9.1 convolution_bitcast_fusion.1
  712.9 92.3 %all-reduce.29.cloned.1.call-done = f32[3072,128]{1,0:T(8,128)} async-done(((f32[3072,128]{1,0:T(8,128)}), f32[3072,128]{1,0:T(8,128)}) %all-reduce.29.cloned.1.call-update) | async-done | bytes 1572880 | tf_op jit(solution)/shard_map/psum | solution.py:22
  815.5 10.3 fusion.4
  825.9 27.6 %all-reduce.31.cloned.1.call-done = bf16[2048,128]{0,1:T(8,128)(2,1)} async-done(((bf16[2048,128]{0,1:T(8,128)(2,1)}), bf16[2048,128]{0,1:T(8,128)(2,1)}) %all-reduce.31.cloned.1.call-update) | async-done | bytes 524304 | tf_op jit(solution)/shard_map/psum | solution.py:33
  854.8 21.6 %all-gather.10 = f32[16,1,128]{2,1,0:T(1,128)S(1)} all-gather(f32[1,1,128]{2,1,0:T(1,128)S(1)} %bitcast.45), channel_id=6, replica_groups=mesh['rows'=16,'cols'=2] {'rows'}, dimensions={0}, use_global_device_ids=true | all-gather | bytes 8704 | tf_op jit(solution)/shard_map/all_gather | solution.py:38
  876.4 11.3 %convolution_bitcast_fusion = f32[3072,128]{1,0:T(8,128)} fusion(bf16[2048,3072]{1,0:T(8,128)(2,1)} %param.3, f32[2048,128]{0,1:T(8,128)} %copy-done.3, bf16[2048,128]{0,1:T(8,128)(2,1)} %all-reduce.31.cloned.1.call-done, f32[128]{0:T(128)S(1)} %div.41), kind=kOutput, calls=%fused_computation | convolution fusion | flops 1611661312 | bytes 15729152 | tf_op jit(solution)/shard_map/dot_general | solution.py:10
  887.8 92.1 %all-reduce.33.cloned.1.call-done = f32[3072,128]{1,0:T(8,128)} async-done(((f32[3072,128]{1,0:T(8,128)}), f32[3072,128]{1,0:T(8,128)}) %all-reduce.33.cloned.1.call-update) | async-done | bytes 1572880 | tf_op jit(solution)/shard_map/psum | solution.py:22
  990.2 10.3 fusion.5
  1000.9 27.3 %all-reduce.35.cloned.1.call-done = bf16[2048,128]{0,1:T(8,128)(2,1)} async-done(((bf16[2048,128]{0,1:T(8,128)(2,1)}), bf16[2048,128]{0,1:T(8,128)(2,1)}) %all-reduce.35.cloned.1.call-update) | async-done | bytes 524304 | tf_op jit(solution)/shard_map/psum | solution.py:33
  1029.5 21.6 %all-gather.11 = f32[16,1,128]{2,1,0:T(1,128)S(1)} all-gather(f32[1,1,128]{2,1,0:T(1,128)S(1)} %bitcast.46), channel_id=7, replica_groups=mesh['rows'=16,'cols'=2] {'rows'}, dimensions={0}, use_global_device_ids=true | all-gather | bytes 8704 | tf_op jit(solution)/shard_map/all_gather | solution.py:38
  1056.6 6.5 fusion.6
  (90 shorter events, 71.5 us)
Async XLA Ops:
  7.2 108.2 %all-reduce.13.cloned.1.call-start = ((), (), s32[]{:S(2)}) async-start(), calls=%async_computation | async-start | bytes 3145728 | tf_op jit(solution)/shard_map/psum | solution.py:22
  16.5 98.9 %copy-start.6 = (f32[3072]{0:T(1024)S(1)}, f32[3072]{0:T(1024)}, u32[]{:S(2)}) copy-start(f32[3072]{0:T(1024)} %param.5) | copy-start | bytes 36868
  16.5 138.8 %all-reduce.15.cloned.1.call-start = ((), (), s32[]{:S(2)}) async-start(), calls=%async_computation.1 | async-start | bytes 1048576 | tf_op jit(solution)/shard_map/psum | solution.py:33
  117.2 10.4 copy-start.7
  127.6 153.9 %all-reduce.17.cloned.1.call-start = ((), (), s32[]{:S(2)}) async-start(), calls=%async_computation.2 | async-start | bytes 3145728 | tf_op jit(solution)/shard_map/psum | solution.py:22
  127.9 61.2 %copy-start.5 = (bf16[2048,128]{0,1:T(8,128)(2,1)}, bf16[2048,128]{0,1:T(8,128)(2,1)S(1)}, u32[]{:S(2)}) copy-start(bf16[2048,128]{0,1:T(8,128)(2,1)S(1)} %copy.13) | copy-start | bytes 1572868
  189.1 139.2 %all-reduce.19.cloned.1.call-start = ((), (), s32[]{:S(2)}) async-start(), calls=%async_computation.3 | async-start | bytes 1048576 | tf_op jit(solution)/shard_map/psum | solution.py:33
  300.6 154.5 %all-reduce.21.cloned.1.call-start = ((), (), s32[]{:S(2)}) async-start(), calls=%async_computation.4 | async-start | bytes 3145728 | tf_op jit(solution)/shard_map/psum | solution.py:22
  362.6 140.3 %all-reduce.23.cloned.1.call-start = ((), (), s32[]{:S(2)}) async-start(), calls=%async_computation.5 | async-start | bytes 1048576 | tf_op jit(solution)/shard_map/psum | solution.py:33
  463.7 1.2 copy-start
  475.2 154.1 %all-reduce.25.cloned.1.call-start = ((), (), s32[]{:S(2)}) async-start(), calls=%async_computation.6 | async-start | bytes 3145728 | tf_op jit(solution)/shard_map/psum | solution.py:22
  537.2 140.5 %all-reduce.27.cloned.1.call-start = ((), (), s32[]{:S(2)}) async-start(), calls=%async_computation.7 | async-start | bytes 1048576 | tf_op jit(solution)/shard_map/psum | solution.py:33
  638.5 1.1 copy-start.1
  650.0 155.2 %all-reduce.29.cloned.1.call-start = ((), (), s32[]{:S(2)}) async-start(), calls=%async_computation.8 | async-start | bytes 3145728 | tf_op jit(solution)/shard_map/psum | solution.py:22
  702.8 1.0 copy-start.3
  712.8 140.7 %all-reduce.31.cloned.1.call-start = ((), (), s32[]{:S(2)}) async-start(), calls=%async_computation.9 | async-start | bytes 1048576 | tf_op jit(solution)/shard_map/psum | solution.py:33
  814.4 1.1 copy-start.2
  825.9 154.0 %all-reduce.33.cloned.1.call-start = ((), (), s32[]{:S(2)}) async-start(), calls=%async_computation.10 | async-start | bytes 3145728 | tf_op jit(solution)/shard_map/psum | solution.py:22
  887.7 140.6 %all-reduce.35.cloned.1.call-start = ((), (), s32[]{:S(2)}) async-start(), calls=%async_computation.11 | async-start | bytes 1048576 | tf_op jit(solution)/shard_map/psum | solution.py:33
  989.0 1.2 copy-start.4
Sparse Core Ops, SparseCore 0:
  16.6 98.6 all-reduce.12
  127.7 27.5 all-reduce.14
  189.2 92.2 all-reduce.16
  300.7 27.5 all-reduce.18
  362.7 92.2 all-reduce.20
  475.3 27.5 all-reduce.22
  537.3 91.9 all-reduce.24
  650.1 27.5 all-reduce.26
  713.0 92.2 all-reduce.28
  826.0 27.5 all-reduce.30
  887.8 91.9 all-reduce.32
  1000.7 27.5 all-reduce.34
